TPU v7x, 32 devices: a whole 2x2x4 slice. The times are simulated.
32 devices in a mesh: gx: 2 (over core), gy: 4 (over y, x), gz: 4 (over z).
Axes of the slice: x: 2, y: 2, z: 4, core: 2. Of those that a mesh axis runs over, the one named last changes fastest.
Arguments:
- raw_weight: float32 [128, 27, 128], P(('gx', 'gy')), may hold values from -6 to 6
- inputs: bfloat16 [16, 64, 64, 128], P('gx', 'gy', 'gz'), may hold values from -6 to 6
- cotangent: bfloat16 [16, 64, 64, 128], P('gx', 'gy', 'gz'), may hold values from -0.099609375 to 0.099609375
Outputs:
- input_grad: bfloat16 [16, 64, 64, 128], P('gx', 'gy', 'gz')
- weight_grad: float32 [128, 27, 128], P(('gx', 'gy'))
All inputs are finite; a program needn't handle non-finite values.
Results may differ from a plain program's by a relative error of at most 0.0049.
Values may be sent and summed in bfloat16 or wider, within the bound.
A program may use at most 64 MiB of HBM per device.

v0:
```python
import jax
import jax.numpy as jnp
from jax import lax
from jax.sharding import PartitionSpec as P

var_eps = 1e-05
norm_eps = 1e-06
clip_norm = 600.0


def with_halo(cells, sides, width):
    for axis, dim in sides:
        count = lax.axis_size(axis)
        ends = count - 1
        head = lax.slice_in_dim(cells, 0, width, axis=dim)
        tail = lax.slice_in_dim(cells, cells.shape[dim] - width, cells.shape[dim], axis=dim)
        cells = jnp.concatenate(
            [
                lax.ppermute(tail, axis, [(i, (i + 1) % count) for i in range(ends)]),
                cells,
                lax.ppermute(head, axis, [((i + 1) % count, i) for i in range(ends)]),
            ],
            axis=dim,
        )
    return cells


def tap_view(padded, tap_a, tap_b, tap_c, extent):
    view = padded[
        2 - tap_a : 2 - tap_a + extent[0],
        2 - tap_b : 2 - tap_b + extent[1],
        2 - tap_c : 2 - tap_c + extent[2],
        :,
    ]
    return view.reshape(-1, view.shape[-1])


def input_rows(padded, extent, block_rows):
    row_count = block_rows.shape[0]
    total = jnp.zeros((extent[0] * extent[1] * extent[2], row_count), jnp.float32)
    for tap_a in range(3):
        for tap_b in range(3):
            for tap_c in range(3):
                tap_index = tap_a * 9 + tap_b * 3 + tap_c
                view = tap_view(padded, tap_a, tap_b, tap_c, extent)
                total = total + lax.dot_general(
                    view,
                    block_rows[:, tap_index, :],
                    (((1,), (1,)), ((), ())),
                    preferred_element_type=jnp.float32,
                )
    return total.astype(jnp.bfloat16).reshape(extent[0], extent[1], extent[2], row_count)


def filter_terms(padded, flat_in, extent):
    pieces = []
    for tap_a in range(3):
        for tap_b in range(3):
            for tap_c in range(3):
                view = tap_view(padded, tap_a, tap_b, tap_c, extent)
                pieces.append(
                    lax.dot_general(
                        flat_in, view, (((0,), (0,)), ((), ())), preferred_element_type=jnp.float32
                    )
                )
    return jnp.stack(pieces, axis=1)


def on_device(raw_weight, inputs, cotangent):
    extent = inputs.shape[:3]
    channels = inputs.shape[3]
    fan_count = channels * raw_weight.shape[1]
    padded = with_halo(cotangent, (("gx", 0), ("gy", 1), ("gz", 2)), 1)
    flat_in = inputs.reshape(-1, channels)
    sum_first, sum_second = lax.psum(
        (jnp.sum(raw_weight, axis=(0, 1)), jnp.sum(raw_weight * raw_weight, axis=(0, 1))),
        ("gx", "gy"),
    )
    mean_out = sum_first / fan_count
    var_out = sum_second / fan_count - mean_out * mean_out
    inv_std = lax.rsqrt(var_out + var_eps)
    std_float = (raw_weight - mean_out) * inv_std
    std_whole = lax.all_gather(std_float.astype(jnp.bfloat16), ("gx", "gy"), axis=0, tiled=True)
    input_grad = input_rows(padded, extent, std_whole)
    local_terms = filter_terms(padded, flat_in, extent)
    column_sum = lax.psum(local_terms, "gz")
    filter_grad = lax.psum_scatter(column_sum, ("gx", "gy"), scatter_dimension=0, tiled=True)
    local_grad = jnp.sum(filter_grad, axis=(0, 1))
    local_cross = jnp.sum(filter_grad * std_float, axis=(0, 1))
    local_square = jnp.sum(filter_grad * filter_grad, axis=(0, 1))
    sum_grad, sum_cross, sum_square = lax.psum(
        (local_grad, local_cross, local_square), ("gx", "gy")
    )
    mean_grad = sum_grad / fan_count
    mean_cross = sum_cross / fan_count
    raw_grad = inv_std * (filter_grad - mean_grad - std_float * mean_cross)
    per_output = sum_square - 2.0 * mean_grad * sum_grad - 2.0 * mean_cross * sum_cross
    per_output = (
        per_output
        + fan_count * mean_grad * mean_grad
        + fan_count * mean_cross * mean_cross * var_out / (var_out + var_eps)
    )
    square_sum = jnp.sum(inv_std * inv_std * per_output)
    scale = jnp.minimum(1.0, clip_norm * lax.rsqrt(square_sum + norm_eps))
    return (input_grad, raw_grad * scale)


def solution(mesh):
    in_specs = (P(("gx", "gy"), None, None), P("gx", "gy", "gz", None), P("gx", "gy", "gz", None))
    out_specs = (P("gx", "gy", "gz", None), P(("gx", "gy"), None, None))
    return jax.shard_map(
        on_device, mesh=mesh, in_specs=in_specs, out_specs=out_specs, check_vma=False
    )
```

profile of v0, /device:TPU:0, one launch (start us, length us, event | category | flops | bytes accessed | tf_op | source)
XLA Modules:
  0.0 215.6 jit_solution(4366381669883090917)
XLA Ops:
  8.2 2.4 %collective-permute-start = (bf16[1,16,16,128]{3,2,1,0:T(8,128)(2,1)S(1)}, bf16[1,16,16,128]{3,2,1,0:T(8,128)(2,1)S(1)}, u32[]{:S(2)}, u32[]{:S(2)}) collective-permute-start(bf16[1,16,16,128]{3,2,1,0:T(8,128)(2,1)S(1)} %get-tuple-element.51), channel_id=1, source_target_pairs={{0,16},{1,17},{2,18},{3,19},{4,20},{5,21},{6,22},{7,23},{8,24},{9,... | collective-permute-start | bytes 196616 | tf_op jit(solution)/shard_map/ppermute | solution.py:19
  10.6 1.3 collective-permute-start.1
  11.9 1.4 constant_dynamic-update-slice_fusion.5
  13.8 1.3 collective-permute-start.3
  15.1 4.8 %collective-permute-start.2 = (bf16[10,1,16,128]{3,2,1,0:T(8,128)(2,1)S(1)}, bf16[10,1,16,128]{3,2,1,0:T(8,128)(2,1)S(1)}, u32[]{:S(2)}, u32[]{:S(2)}) collective-permute-start(bf16[10,1,16,128]{3,2,1,0:T(8,128)(2,1)S(1)} %get-tuple-element.45), channel_id=1, source_target_pairs={{0,4},{4,8},{8,12},{1,5},{5,9},{9,13},{2,6},{6,10},{10,14},{3,7},{... | collective-permute-start | bytes 122888 | tf_op jit(solution)/shard_map/ppermute | solution.py:19
  20.3 1.3 collective-permute-done.2
  21.8 1.3 collective-permute-start.4
  23.1 4.6 %collective-permute-start.5 = (bf16[10,18,1,128]{3,2,1,0:T(2,128)(2,1)S(1)}, bf16[10,18,1,128]{3,2,1,0:T(2,128)(2,1)S(1)}, u32[]{:S(2)}, u32[]{:S(2)}) collective-permute-start(bf16[10,18,1,128]{3,2,1,0:T(2,128)(2,1)S(1)} %get-tuple-element.35), channel_id=1, source_target_pairs={{0,1},{1,2},{2,3},{4,5},{5,6},{6,7},{8,9},{9,10},{10,11},{12,13},{... | collective-permute-start | bytes 138248 | tf_op jit(solution)/shard_map/ppermute | solution.py:19
  28.3 1.5 collective-permute-done.5
  30.6 1.0 fusion.29
  31.6 1.0 fusion.10
  32.6 1.0 fusion.28
  33.5 1.0 fusion.27
  34.5 1.0 fusion.9
  35.5 1.0 fusion.26
  36.5 1.0 fusion.25
  37.4 1.0 fusion.8
  38.4 1.0 fusion.24
  39.4 1.0 fusion.23
  40.4 1.0 fusion.7
  42.3 1.0 fusion.21
  43.3 1.0 fusion.20
  44.3 1.0 fusion.19
  45.3 1.0 fusion.18
  46.3 1.0 fusion.6
  47.2 1.0 fusion.17
  48.2 1.0 fusion.16
  51.1 1.0 fusion.14
  52.1 1.0 fusion.4
  53.1 1.0 fusion.13
  54.1 1.0 fusion.12
  55.0 1.0 fusion.3
  56.0 1.0 fusion.11
  57.0 3.1 %copy.12 = f32[128,27,128]{2,1,0:T(8,128)} copy(f32[128,27,128]{0,2,1:T(8,128)} %fusion.11) | data formatting | bytes 3538944 | tf_op jit(solution)/shard_map/stack | solution.py:66
  60.2 1.0 multiply_reduce_fusion.2
  61.2 16.7 %all-reduce.1 = (f32[128]{0:T(128)S(1)}, f32[128]{0:T(128)S(1)}) all-reduce(f32[128]{0:T(128)S(1)} %get-tuple-element.8, f32[128]{0:T(128)S(1)} %get-tuple-element.7), channel_id=1, replica_groups=mesh['gx'=2,'gy'=4,'gz'=4] {'gx','gy'}, use_global_device_ids=true, to_apply=%region_1.0 | all-reduce | flops 256 | bytes 2048 | tf_op jit(solution)/shard_map/psum | solution.py:75
  77.9 1.9 slice.299
  79.8 1.9 slice.338
  81.7 1.7 fusion.32
  83.4 22.2 %reduce-scatter.2.cloned.1.call-done = f32[16,27,128]{2,1,0:T(8,128)} async-done(((f32[128,27,128]{2,1,0:T(8,128)}), f32[16,27,128]{2,1,0:T(8,128)}) %reduce-scatter.2.cloned.1.call-update) | async-done | bytes 221200 | tf_op jit(solution)/shard_map/reduce_scatter | solution.py:87
  105.6 1.8 copy.13
  107.4 3.7 %fusion.65 = (bf16[8,16,16,128]{3,2,1,0:T(8,128)(2,1)}, bf16[8,16,16,128]{3,2,1,0:T(8,128)(2,1)}, bf16[8,16,16,128]{3,2,1,0:T(8,128)(2,1)}, bf16[8,16,16,128]{3,...) fusion(bf16[10,18,17,128]{3,2,1,0:T(8,128)(2,1)S(1)} %get-tuple, ...), kind=kLoop, calls=%fused_computation.177 | loop fusion | bytes 18874368 | tf_op jit(solution)/shard_map/slice | solution.py:29
  111.1 32.5 %all-reduce.4.cloned.1.call-done = f32[16,27,128]{2,0,1:T(8,128)} async-done(((f32[16,27,128]{2,0,1:T(8,128)}), f32[16,27,128]{2,0,1:T(8,128)}) %all-reduce.4.cloned.1.call-update) | async-done | bytes 221200 | tf_op jit(solution)/shard_map/psum | solution.py:86
  143.6 1.1 multiply_reduce_fusion
  144.8 14.4 %all-reduce = (f32[128]{0:T(128)S(1)}, f32[128]{0:T(128)S(1)}, f32[128]{0:T(128)S(1)}) all-reduce(f32[128]{0:T(128)S(1)} %get-tuple-element.5, f32[128]{0:T(128)S(1)} %get-tuple-element.6, f32[128]{0:T(128)S(1)} %get-tuple-element.4), channel_id=1, replica_groups=mesh['gx'=2,'gy'=4,'gz'=4] {'gx','gy'}, use_global_device_ids=true, to_apply=%region_9.0 | all-reduce | flops 384 | bytes 3072 | tf_op jit(solution)/shard_map/psum | solution.py:91
  160.5 1.8 multiply_multiply_fusion
  162.3 27.9 %all_gather.3 = bf16[128,27,128]{2,0,1:T(8,128)(2,1)S(1)} all-gather(bf16[16,27,128]{2,0,1:T(8,128)(2,1)S(1)} %get-tuple-element.53), channel_id=1, replica_groups=mesh['gx'=2,'gy'=4,'gz'=4] {'gx','gy'}, dimensions={0}, use_global_device_ids=true | all-gather | bytes 995328 | tf_op jit(solution)/shard_map/all_gather | solution.py:83
  207.7 1.1 fusion.2
  (105 shorter events, 24.2 us)
Async XLA Ops:
  7.2 23.5 %copy-start = (bf16[8,16,16,128]{3,2,1,0:T(8,128)(2,1)S(1)}, bf16[8,16,16,128]{3,2,1,0:T(8,128)(2,1)}, u32[]{:S(2)}) copy-start(bf16[8,16,16,128]{3,2,1,0:T(8,128)(2,1)} %param.4) | copy-start | bytes 1572868
  7.2 98.4 %reduce-scatter.2.cloned.1.call-start = ((), (), s32[]{:S(2)}) async-start(), calls=%async_computation.1 | async-start | bytes 2359296 | tf_op jit(solution)/shard_map/reduce_scatter | solution.py:87
  8.2 3.7 %collective-permute-start = (bf16[1,16,16,128]{3,2,1,0:T(8,128)(2,1)S(1)}, bf16[1,16,16,128]{3,2,1,0:T(8,128)(2,1)S(1)}, u32[]{:S(2)}, u32[]{:S(2)}) collective-permute-start(bf16[1,16,16,128]{3,2,1,0:T(8,128)(2,1)S(1)} %get-tuple-element.51), channel_id=1, source_target_pairs={{0,16},{1,17},{2,18},{3,19},{4,20},{5,21},{6,22},{7,23},{8,24},{9,... | collective-permute-start | bytes 196616 | tf_op jit(solution)/shard_map/ppermute | solution.py:19
  10.6 3.1 %collective-permute-start.1 = (bf16[1,16,16,128]{3,2,1,0:T(8,128)(2,1)S(1)}, bf16[1,16,16,128]{3,2,1,0:T(8,128)(2,1)S(1)}, u32[]{:S(2)}, u32[]{:S(2)}) collective-permute-start(bf16[1,16,16,128]{3,2,1,0:T(8,128)(2,1)S(1)} %get-tuple-element.50), channel_id=1, source_target_pairs={{16,0},{17,1},{18,2},{19,3},{20,4},{21,5},{22,6},{23,7},{24,8},{25... | collective-permute-start | bytes 196616 | tf_op jit(solution)/shard_map/ppermute | solution.py:21
  13.3 38.8 %copy-start.29 = (bf16[9,16,16,128]{3,2,1,0:T(8,128)(2,1)}, bf16[9,16,16,128]{3,2,1,0:T(8,128)(2,1)S(1)}, u32[]{:S(2)}) copy-start(bf16[9,16,16,128]{3,2,1,0:T(8,128)(2,1)S(1)} %get-tuple-element.47) | copy-start | bytes 1769476
  13.7 20.8 %copy-start.28 = (bf16[9,16,16,128]{3,2,1,0:T(8,128)(2,1)}, bf16[9,16,16,128]{3,2,1,0:T(8,128)(2,1)S(1)}, u32[]{:S(2)}) copy-start(bf16[9,16,16,128]{3,2,1,0:T(8,128)(2,1)S(1)} %get-tuple-element.56) | copy-start | bytes 1769476
  13.8 6.6 %collective-permute-start.3 = (bf16[10,1,16,128]{3,2,1,0:T(8,128)(2,1)S(1)}, bf16[10,1,16,128]{3,2,1,0:T(8,128)(2,1)S(1)}, u32[]{:S(2)}, u32[]{:S(2)}) collective-permute-start(bf16[10,1,16,128]{3,2,1,0:T(8,128)(2,1)S(1)} %get-tuple-element.46), channel_id=1, source_target_pairs={{4,0},{8,4},{12,8},{5,1},{9,5},{13,9},{6,2},{10,6},{14,10},{7,3},{... | collective-permute-start | bytes 122888 | tf_op jit(solution)/shard_map/ppermute | solution.py:21
  15.1 6.6 %collective-permute-start.2 = (bf16[10,1,16,128]{3,2,1,0:T(8,128)(2,1)S(1)}, bf16[10,1,16,128]{3,2,1,0:T(8,128)(2,1)S(1)}, u32[]{:S(2)}, u32[]{:S(2)}) collective-permute-start(bf16[10,1,16,128]{3,2,1,0:T(8,128)(2,1)S(1)} %get-tuple-element.45), channel_id=1, source_target_pairs={{0,4},{4,8},{8,12},{1,5},{5,9},{9,13},{2,6},{6,10},{10,14},{3,7},{... | collective-permute-start | bytes 122888 | tf_op jit(solution)/shard_map/ppermute | solution.py:19
  21.8 6.5 %collective-permute-start.4 = (bf16[10,18,1,128]{3,2,1,0:T(2,128)(2,1)S(1)}, bf16[10,18,1,128]{3,2,1,0:T(2,128)(2,1)S(1)}, u32[]{:S(2)}, u32[]{:S(2)}) collective-permute-start(bf16[10,18,1,128]{3,2,1,0:T(2,128)(2,1)S(1)} %get-tuple-element.34), channel_id=1, source_target_pairs={{1,0},{2,1},{3,2},{5,4},{6,5},{7,6},{9,8},{10,9},{11,10},{13,12},{... | collective-permute-start | bytes 138248 | tf_op jit(solution)/shard_map/ppermute | solution.py:21
  23.1 6.7 %collective-permute-start.5 = (bf16[10,18,1,128]{3,2,1,0:T(2,128)(2,1)S(1)}, bf16[10,18,1,128]{3,2,1,0:T(2,128)(2,1)S(1)}, u32[]{:S(2)}, u32[]{:S(2)}) collective-permute-start(bf16[10,18,1,128]{3,2,1,0:T(2,128)(2,1)S(1)} %get-tuple-element.35), channel_id=1, source_target_pairs={{0,1},{1,2},{2,3},{4,5},{5,6},{6,7},{8,9},{9,10},{10,11},{12,13},{... | collective-permute-start | bytes 138248 | tf_op jit(solution)/shard_map/ppermute | solution.py:19
  42.3 1.0 copy-start.1
  60.2 83.5 %all-reduce.4.cloned.1.call-start = ((), (), s32[]{:S(2)}) async-start(), calls=%async_computation.2 | async-start | bytes 442368 | tf_op jit(solution)/shard_map/psum | solution.py:86
  144.8 45.7 %copy-start.22 = (bf16[8,16,16,128]{3,2,1,0:T(8,128)(2,1)S(1)}, bf16[8,16,16,128]{3,2,1,0:T(8,128)(2,1)}, u32[]{:S(2)}) copy-start(bf16[8,16,16,128]{3,2,1,0:T(8,128)(2,1)} %get-tuple-element.43) | copy-start | bytes 1572868
  190.1 1.0 copy-start.20
  190.4 1.1 copy-start.19
  191.5 1.1 copy-start.18
  191.8 1.1 copy-start.3
  192.9 1.0 copy-start.17
  193.2 1.1 copy-start.27
  194.2 1.1 copy-start.16
  194.6 1.1 copy-start.15
  195.6 1.1 copy-start.26
  196.0 1.1 copy-start.14
  197.0 1.1 copy-start.13
  197.4 1.1 copy-start.2
  198.3 1.1 copy-start.12
  198.7 1.1 copy-start.11
  199.7 1.1 copy-start.25
  200.1 1.1 copy-start.10
  201.1 1.1 copy-start.9
  201.5 1.1 copy-start.24
  202.4 1.1 copy-start.8
  202.9 1.1 copy-start.7
  203.8 1.1 copy-start.21
  204.3 1.1 copy-start.6
  205.2 1.1 copy-start.5
  205.6 1.1 copy-start.23
  206.6 1.1 copy-start.4
Sparse Core Ops, SparseCore 0:
  60.3 45.2 reduce-scatter.1
  108.5 35.0 all-reduce.3
where the time goes:
time: 217 us; the launch traced here: 216 us
  waiting for transfers between devices  59 us (27%)
  blocking collectives  58.9 us (27%)
  matrix products  35 us (16%)
  local copies, waits for them, and re-layouts  24.4 us (11%)
  starting transfers between devices  15.8 us (7%)
  between operations  15.2 us (7%)
  other arithmetic  7.2 us (3%)
    psum x1, waiting for transfers between devices, on_device(): column_sum = lax.psum(local_terms, 'gz')  32.5 us
    all_gather x1, blocking collectives, on_device(): lax.all_gather(std_float.astype(jnp.bfloat16), ('gx', 'gy'), axis=0, tile...  27.9 us
    dot_general x27, matrix products, filter_terms(): lax.dot_general(flat_in, view, (((0,), (0,)), ((), ())), preferred_elemen...  26.3 us
    reduce_scatter x1, waiting for transfers between devices, on_device(): lax.psum_scatter(column_sum, ('gx', 'gy'), scatter_dimension=0, tiled=True)  22.2 us
    psum x1, blocking collectives, on_device(): lax.psum((jnp.sum(raw_weight, axis=(0, 1)), jnp.sum(raw_weight * raw_weig...  16.7 us
    psum x1, blocking collectives, on_device(): lax.psum((local_grad, local_cross, local_square), ('gx', 'gy'))  14.4 us
    ppermute x3, starting transfers between devices, with_halo(): lax.ppermute(tail, axis, [(i, (i + 1) % count) for i in range(ends)])  11.8 us
    unnamed x61, local copies, waits for them, and re-layouts  9.64 us
  transfers between devices with their start and end apart: 8, of which 7 were waited for; matrix products, arithmetic and copies ran while one was open for 5% of the time, Pallas kernels for 0%

commit v1 on v0

v1 whole, which is shorter than its diff:
```python
import functools

import jax
import jax.numpy as jnp
from jax import lax
from jax.experimental import pallas as pl
from jax.experimental.pallas import tpu as pltpu
from jax.sharding import PartitionSpec as P

var_eps = 1e-05
norm_eps = 1e-06
clip_norm = 600.0
F32 = jnp.float32
BF16 = jnp.bfloat16
MESH = pl.DeviceIdType.MESH
AXES = ("gx", "gy", "gz")


def kernel(dims, raw_ref, in_ref, cot_ref, dx_ref, wg_ref, *scratch):
    (shifted, face_out, face_in, in_t, part, recv_x, send_y, recv_y, send_z, recv_z, full, std,
     std_all, w_cat, stats, stats_in, halo_send, halo_recv, x_send, x_recv, y_send, y_recv,
     z_send, z_recv, g_send, g_recv, ay_send, ay_recv, ax_send, ax_recv, st_send, st_recv) = scratch
    count = dict(zip(AXES, dims))
    nx, ny, nz = dims
    me = {axis: lax.axis_index(axis) for axis in AXES}
    rows, taps, chan = raw_ref.shape
    ex, ey, ez = in_ref.shape[:3]
    piece = part.shape[2] // nz
    fan_count = float(rows * nx * ny * taps)

    def peer(axis, k):
        return lax.rem(me[axis] + k, count[axis])

    def remote(src, dst, send_sem, recv_sem, axis, where):
        return pltpu.make_async_remote_copy(
            src_ref=src, dst_ref=dst, send_sem=send_sem, recv_sem=recv_sem,
            device_id={axis: where}, device_id_type=MESH,
        )

    def wait_all(copies):
        for copy in copies:
            copy.wait()

    barrier = pltpu.get_barrier_semaphore()
    for axis in AXES:
        for k in range(1, count[axis]):
            pl.semaphore_signal(barrier, inc=1, device_id={axis: peer(axis, k)}, device_id_type=MESH)

    def exchange_start(slot, axis):
        base = (slot * 2 + (0 if axis == "gx" else 1)) * (max(dims) - 1)
        copies = []
        for k in range(1, count[axis]):
            copy = remote(stats.at[slot * 2 + (0 if axis == "gx" else 1)], stats_in.at[base + k - 1],
                          st_send.at[base + k - 1], st_recv.at[base + k - 1], axis, peer(axis, k))
            copy.start()
            copies.append(copy)
        return copies

    def exchange_sum(slot, axis):
        index = slot * 2 + (0 if axis == "gx" else 1)
        base = index * (max(dims) - 1)
        total = stats[index]
        for k in range(1, count[axis]):
            total = total + stats_in[base + k - 1]
        return total

    raw = raw_ref[...]
    first = jnp.sum(jnp.sum(raw, axis=0), axis=0, keepdims=True)
    second = jnp.sum(jnp.sum(raw * raw, axis=0), axis=0, keepdims=True)
    pad = jnp.zeros((6, chan), F32)
    stats[0] = jnp.concatenate([first, second, pad], axis=0)

    zero_plane = jnp.zeros((ey, ez, chan), BF16)
    zero_col = jnp.zeros((ex + 2, ez, chan), BF16)
    zero_face = jnp.zeros((ex + 2, ey + 2, chan), BF16)

    @pl.when(me["gx"] == 0)
    def _():
        shifted[1, 0, 1:ey + 1] = zero_plane

    @pl.when(me["gx"] == nx - 1)
    def _():
        shifted[1, ex + 1, 1:ey + 1] = zero_plane

    @pl.when(me["gy"] == 0)
    def _():
        shifted[1, :, 0] = zero_col

    @pl.when(me["gy"] == ny - 1)
    def _():
        shifted[1, :, ey + 1] = zero_col

    @pl.when(me["gz"] == 0)
    def _():
        face_in[0] = zero_face

    @pl.when(me["gz"] == nz - 1)
    def _():
        face_in[1] = zero_face

    pl.semaphore_wait(barrier, sum(n - 1 for n in dims))

    def halo(axis, number, low_src, high_dst, high_src, low_dst):
        lower, upper = lax.max(me[axis] - 1, 0), lax.min(me[axis] + 1, count[axis] - 1)
        down = remote(low_src, high_dst, halo_send.at[2 * number], halo_recv.at[2 * number], axis, lower)
        up = remote(high_src, low_dst, halo_send.at[2 * number + 1], halo_recv.at[2 * number + 1], axis, upper)

        @pl.when(me[axis] > 0)
        def _():
            down.start()

        @pl.when(me[axis] < count[axis] - 1)
        def _():
            up.start()

        def finish():
            @pl.when(me[axis] > 0)
            def _():
                down.wait_send()
                up.wait_recv()

            @pl.when(me[axis] < count[axis] - 1)
            def _():
                up.wait_send()
                down.wait_recv()

        return finish

    body = pl.ds(1, ey)
    halo_x = halo("gx", 0, cot_ref.at[0], shifted.at[1, ex + 1, body],
                  cot_ref.at[ex - 1], shifted.at[1, 0, body])
    stats_x = exchange_start(0, "gx")
    shifted[1, 1:ex + 1, 1:ey + 1] = cot_ref[...]
    halo_x()
    halo_y = halo("gy", 1, shifted.at[1, :, 1], shifted.at[1, :, ey + 1],
                  shifted.at[1, :, ey], shifted.at[1, :, 0])
    wait_all(stats_x)
    stats[1] = exchange_sum(0, "gx")
    stats_y = exchange_start(0, "gy")
    for x in range(ex):
        in_t[:, x * ey * ez:(x + 1) * ey * ez] = in_ref[x].reshape(ey * ez, chan).T
    halo_y()
    for x in range(ex + 2):
        plane = shifted[1, x].astype(F32)
        face_out[0, x] = plane[:, 0, :].astype(BF16)
        face_out[1, x] = plane[:, ez - 1, :].astype(BF16)
    halo_z = halo("gz", 2, face_out.at[0], face_in.at[1], face_out.at[1], face_in.at[0])

    wait_all(stats_y)
    sums = exchange_sum(0, "gy")
    mean_out = sums[0:1] / fan_count
    var_out = sums[1:2] / fan_count - mean_out * mean_out
    inv_std = lax.rsqrt(var_out + var_eps)
    own = std_all.at[me["gx"], me["gy"]]
    for t in range(taps):
        value = (raw_ref[:, t, :] - mean_out) * inv_std
        std[t] = value
        own[t] = value.astype(BF16)
    gather_y = []
    for k in range(1, ny):
        copy = remote(own, own, ay_send.at[k - 1], ay_recv.at[k - 1], "gy", peer("gy", k))
        copy.start()
        gather_y.append(copy)

    halo_z()
    depth_index = lax.broadcasted_iota(jnp.int32, (ey + 2, ez, chan), 1)
    for x in range(ex + 2):
        plane = shifted[1, x].astype(F32)
        low = face_in[0, x].astype(F32)[:, None, :]
        high = face_in[1, x].astype(F32)[:, None, :]
        shifted[0, x] = jnp.where(depth_index == 0, low, pltpu.roll(plane, 1, 1)).astype(BF16)
        shifted[2, x] = jnp.where(depth_index == ez - 1, high, pltpu.roll(plane, ez - 1, 1)).astype(BF16)

    def view(t, start, planes):
        a, b, c = t // 9, (t // 3) % 3, t % 3
        block = shifted[2 - c, pl.ds(start + 2 - a, planes), 2 - b:2 - b + ey]
        return block.reshape(planes * ey * ez, chan)

    for t in range(0, taps, 2):
        group = list(range(t, min(t + 2, taps)))
        right = jnp.concatenate([view(s, 0, ex) for s in group], axis=1) if len(group) > 1 else view(t, 0, ex)
        product = jnp.dot(in_t[...], right, preferred_element_type=F32)
        for j, s in enumerate(group):
            for gx in range(nx):
                for gy in range(ny):
                    low = (gx * ny + gy) * rows
                    part[gx, gy, s] = product[low:low + rows, j * chan:(j + 1) * chan]
    for t in range(taps, piece * nz):
        for gx in range(nx):
            for gy in range(ny):
                part[gx, gy, t] = jnp.zeros((rows, chan), F32)
    reduce_x = []
    for k in range(1, nx):
        copy = remote(part.at[peer("gx", k)], recv_x.at[k - 1], x_send.at[k - 1], x_recv.at[k - 1], "gx", peer("gx", k))
        copy.start()
        reduce_x.append(copy)

    wait_all(gather_y)
    gather_x = []
    for k in range(1, nx):
        copy = remote(std_all.at[me["gx"]], std_all.at[me["gx"]], ax_send.at[k - 1], ax_recv.at[k - 1], "gx", peer("gx", k))
        copy.start()
        gather_x.append(copy)

    wait_all(reduce_x)
    for gy in range(ny):
        total = part[me["gx"], gy]
        for k in range(1, nx):
            total = total + recv_x[k - 1, gy]
        send_y[gy] = total.astype(BF16)
    reduce_y = []
    for k in range(1, ny):
        copy = remote(send_y.at[peer("gy", k)], recv_y.at[k - 1], y_send.at[k - 1], y_recv.at[k - 1], "gy", peer("gy", k))
        copy.start()
        reduce_y.append(copy)

    wait_all(gather_x)
    for t in range(taps):
        w_cat[:, t * chan:(t + 1) * chan] = std_all[:, :, t].reshape(nx * ny * rows, chan)
    step = 2 if ex % 2 == 0 else 1

    def dx_step(n, carry):
        start = n * step
        left = jnp.concatenate([view(t, start, step) for t in range(taps)], axis=1)
        product = lax.dot_general(left, w_cat[...], (((1,), (1,)), ((), ())), preferred_element_type=F32)
        dx_ref[pl.ds(start, step)] = product.astype(BF16).reshape(step, ey, ez, chan)
        return carry

    half = ex // step // 2
    lax.fori_loop(0, half, dx_step, 0)

    wait_all(reduce_y)
    total = send_y[me["gy"]].astype(F32)
    for k in range(1, ny):
        total = total + recv_y[k - 1].astype(F32)
    send_z[...] = total.astype(BF16)
    reduce_z = []
    for k in range(1, nz):
        copy = remote(send_z.at[pl.ds(peer("gz", k) * piece, piece)], recv_z.at[k - 1], z_send.at[k - 1], z_recv.at[k - 1], "gz", peer("gz", k))
        copy.start()
        reduce_z.append(copy)

    lax.fori_loop(half, ex // step, dx_step, 0)

    wait_all(reduce_z)
    mine = pl.ds(me["gz"] * piece, piece)
    total = send_z[mine].astype(F32)
    for k in range(1, nz):
        total = total + recv_z[k - 1].astype(F32)
    full[mine] = total
    gather_z = []
    for k in range(1, nz):
        copy = remote(full.at[mine], full.at[mine], g_send.at[k - 1], g_recv.at[k - 1], "gz", peer("gz", k))
        copy.start()
        gather_z.append(copy)
    wait_all(gather_z)

    grad = full[0:taps]
    std_value = std[...]

    def per_output(value):
        return jnp.sum(jnp.sum(value, axis=0), axis=0, keepdims=True)

    stats[2] = jnp.concatenate(
        [per_output(grad), per_output(grad * std_value), per_output(grad * grad), jnp.zeros((5, chan), F32)], axis=0
    )
    wait_all(exchange_start(1, "gx"))
    stats[3] = exchange_sum(1, "gx")
    wait_all(exchange_start(1, "gy"))
    sums = exchange_sum(1, "gy")
    sum_grad, sum_cross, sum_square = sums[0:1], sums[1:2], sums[2:3]
    mean_grad = sum_grad / fan_count
    mean_cross = sum_cross / fan_count
    spread = sum_square - 2.0 * mean_grad * sum_grad - 2.0 * mean_cross * sum_cross
    spread = (
        spread
        + fan_count * mean_grad * mean_grad
        + fan_count * mean_cross * mean_cross * var_out / (var_out + var_eps)
    )
    square_sum = jnp.sum(inv_std * inv_std * spread, axis=1, keepdims=True)
    scale = jnp.minimum(1.0, clip_norm * lax.rsqrt(square_sum + norm_eps))
    factor = inv_std * scale
    for t in range(taps):
        wg_ref[:, t, :] = factor * (full[t] - mean_grad - std[t] * mean_cross)


def on_device(dims, raw_weight, inputs, cotangent):
    nx, ny, nz = dims
    rows, taps, chan = raw_weight.shape
    ex, ey, ez = inputs.shape[:3]
    padded_taps = -(-taps // nz) * nz
    piece = padded_taps // nz
    most = max(dims) - 1
    dma = pltpu.SemaphoreType.DMA

    def pair(n):
        return [dma((max(n, 1),)), dma((max(n, 1),))]

    scratch = [
        pltpu.VMEM((3, ex + 2, ey + 2, ez, chan), BF16),
        pltpu.VMEM((2, ex + 2, ey + 2, chan), BF16),
        pltpu.VMEM((2, ex + 2, ey + 2, chan), BF16),
        pltpu.VMEM((chan, ex * ey * ez), BF16),
        pltpu.VMEM((nx, ny, padded_taps, rows, chan), F32),
        pltpu.VMEM((nx - 1, ny, padded_taps, rows, chan), F32),
        pltpu.VMEM((ny, padded_taps, rows, chan), BF16),
        pltpu.VMEM((ny - 1, padded_taps, rows, chan), BF16),
        pltpu.VMEM((padded_taps, rows, chan), BF16),
        pltpu.VMEM((nz - 1, piece, rows, chan), BF16),
        pltpu.VMEM((padded_taps, rows, chan), F32),
        pltpu.VMEM((taps, rows, chan), F32),
        pltpu.VMEM((nx, ny, taps, rows, chan), BF16),
        pltpu.VMEM((chan, taps * chan), BF16),
        pltpu.VMEM((4, 8, chan), F32),
        pltpu.VMEM((4 * most, 8, chan), F32),
        *pair(6), *pair(nx - 1), *pair(ny - 1), *pair(nz - 1), *pair(nz - 1),
        *pair(ny - 1), *pair(nx - 1), *pair(4 * most),
    ]
    vmem = pl.BlockSpec(memory_space=pltpu.VMEM)
    return pl.pallas_call(
        functools.partial(kernel, dims),
        out_shape=(
            jax.ShapeDtypeStruct(cotangent.shape, BF16),
            jax.ShapeDtypeStruct(raw_weight.shape, F32),
        ),
        in_specs=[vmem] * 3,
        out_specs=(vmem, vmem),
        scratch_shapes=scratch,
        compiler_params=pltpu.CompilerParams(
            collective_id=0, has_side_effects=True, vmem_limit_bytes=48 * 1024 * 1024
        ),
    )(raw_weight, inputs, cotangent)


def solution(mesh):
    dims = tuple(mesh.shape[axis] for axis in AXES)
    in_specs = (P(("gx", "gy"), None, None), P("gx", "gy", "gz", None), P("gx", "gy", "gz", None))
    out_specs = (P("gx", "gy", "gz", None), P(("gx", "gy"), None, None))
    return jax.shard_map(
        functools.partial(on_device, dims), mesh=mesh, in_specs=in_specs, out_specs=out_specs, check_vma=False
    )
```

time: 217 us -> 45.8 us (0.21)
  waiting for transfers between devices: 59 us -> 0 us
  blocking collectives: 58.9 us -> 0 us
  Pallas kernels: 0 us -> 40.2 us
  matrix products: 35 us -> 0 us
  local copies, waits for them, and re-layouts: 24.4 us -> 4.7 us
  starting transfers between devices: 15.8 us -> 0 us
  between operations: 15.2 us -> 0.65 us
  other arithmetic: 7.2 us -> 0 us
    pallas_call x0 -> x1, Pallas kernels: none -> 40.2 us  [on_device(): pl.pallas_call(functools.partial(kernel, dims), out_shape=(jax.ShapeDtype...]
    dot_general x54 -> x0, matrix products: 35 us -> none  [the longest x27 26.3 us: filter_terms(): lax.dot_general(flat_in, view, (((0,), (0,)), ((), ())), preferred_elemen...]
    psum x1 -> x0, waiting for transfers between devices: 32.5 us -> none  [on_device(): column_sum = lax.psum(local_terms, 'gz')]
    psum x2 -> x0, blocking collectives: 31 us -> none  [the longest x1 16.7 us: on_device(): lax.psum((jnp.sum(raw_weight, axis=(0, 1)), jnp.sum(raw_weight * raw_weig...]
    all_gather x1 -> x0, blocking collectives: 27.9 us -> none  [on_device(): lax.all_gather(std_float.astype(jnp.bfloat16), ('gx', 'gy'), axis=0, tile...]
    reduce_scatter x1 -> x0, waiting for transfers between devices: 22.2 us -> none  [on_device(): lax.psum_scatter(column_sum, ('gx', 'gy'), scatter_dimension=0, tiled=True)]
    ppermute x6 -> x0, starting transfers between devices: 15.7 us -> none  [the longest x3 11.8 us: with_halo(): lax.ppermute(tail, axis, [(i, (i + 1) % count) for i in range(ends)])]
    slice x5 -> x0, local copies, waits for them, and re-layouts: 8.46 us -> none  [the longest x3 7.52 us: tap_view(): padded[2 - tap_a:2 - tap_a + extent[0], 2 - tap_b:2 - tap_b + extent[1],...]
  transfers between devices with their start and end apart: 8 -> 0, of which waited for: 7 -> 0; matrix products, arithmetic and copies ran while one was open for 5% -> 0% of each run, Pallas kernels for 0% -> 0%
where the time goes in v1:
time: 45.8 us; the launch traced here: 45.5 us
  Pallas kernels  40.2 us (88%)
  local copies, waits for them, and re-layouts  4.7 us (10%)
  between operations  0.65 us (1%)
    pallas_call x1, Pallas kernels, on_device(): pl.pallas_call(functools.partial(kernel, dims), out_shape=(jax.ShapeDtype...  40.2 us
    unnamed x6, local copies, waits for them, and re-layouts  3.88 us

profile of v1, /device:TPU:0, one launch (start us, length us, event | category | flops | bytes accessed | tf_op | source)
XLA Modules:
  0.0 45.5 jit_solution(16535795546736913477)
XLA Ops:
  0.6 1.0 %copy.5.raw_ref = f32[16,27,128]{2,1,0:T(8,128)S(1)} copy(f32[16,27,128]{2,0,1:T(8,128)} %param.3) | data formatting | bytes 442368 | tf_op args[0]
  1.6 0.0 copy-start
  1.7 1.0 %copy-done = bf16[8,16,16,128]{3,2,1,0:T(8,128)(2,1)S(1)} copy-done((bf16[8,16,16,128]{3,2,1,0:T(8,128)(2,1)S(1)}, bf16[8,16,16,128]{3,2,1,0:T(8,128)(2,1)}, u32[]{:S(2)}) %copy-start) | copy-done | bytes 524312
  2.7 0.0 copy-start.1
  2.7 1.0 %copy-done.1 = bf16[8,16,16,128]{3,2,1,0:T(8,128)(2,1)S(1)} copy-done((bf16[8,16,16,128]{3,2,1,0:T(8,128)(2,1)S(1)}, bf16[8,16,16,128]{3,2,1,0:T(8,128)(2,1)}, u32[]{:S(2)}) %copy-start.1) | copy-done | bytes 524312
  3.7 40.2 %shard_map.50 = (bf16[8,16,16,128]{3,2,1,0:T(8,128)(2,1)S(1)}, f32[16,27,128]{2,1,0:T(8,128)S(1)}) custom-call(f32[16,27,128]{2,1,0:T(8,128)S(1)} %copy.5.raw_ref, bf16[8,16,16,128]{3,2,1,0:T(8,128)(2,1)S(1)} %copy-done, bf16[8,16,16,128]{3,2,1,0:T(8,128)(2,1)S(1)} %copy-done.1), custom_call_target="tpu_custom_call" | custom-call | tf_op jit(solution)/shard_map/pallas_call | solution.py:320
  43.9 0.8 %copy.6 = f32[16,27,128]{2,0,1:T(8,128)} copy(f32[16,27,128]{2,1,0:T(8,128)S(1)} %get-tuple-element.3) | data formatting | bytes 442368 | tf_op jit(solution)/shard_map/pallas_call | solution.py:320
  44.7 0.8 %copy.8 = bf16[8,16,16,128]{3,2,1,0:T(8,128)(2,1)} copy(bf16[8,16,16,128]{3,2,1,0:T(8,128)(2,1)S(1)} %get-tuple-element.6) | data formatting | bytes 1048576
Async XLA Ops:
  1.6 1.0 %copy-start = (bf16[8,16,16,128]{3,2,1,0:T(8,128)(2,1)S(1)}, bf16[8,16,16,128]{3,2,1,0:T(8,128)(2,1)}, u32[]{:S(2)}) copy-start(bf16[8,16,16,128]{3,2,1,0:T(8,128)(2,1)} %in_ref.1) | copy-start | bytes 1572868
  2.7 1.0 %copy-start.1 = (bf16[8,16,16,128]{3,2,1,0:T(8,128)(2,1)S(1)}, bf16[8,16,16,128]{3,2,1,0:T(8,128)(2,1)}, u32[]{:S(2)}) copy-start(bf16[8,16,16,128]{3,2,1,0:T(8,128)(2,1)} %cot_ref.1) | copy-start | bytes 1572868

commit v2 on v1

v2 whole, which is shorter than its diff:
```python
import functools

import jax
import jax.numpy as jnp
from jax import lax
from jax.experimental import pallas as pl
from jax.experimental.pallas import tpu as pltpu
from jax.sharding import PartitionSpec as P

var_eps = 1e-05
norm_eps = 1e-06
clip_norm = 600.0
F32 = jnp.float32
BF16 = jnp.bfloat16
MESH = pl.DeviceIdType.MESH
AXES = ("gx", "gy", "gz")


def kernel(dims, raw_hbm, in_hbm, cot_hbm, dx_ref, wg_ref, *scratch):
    (raw_ref, in_ref, shifted, face_out, face_in, in_t, part, recv_x, send_y, recv_y, send_z, recv_z, full, std,
     std_all, w_cat, stats, stats_in, load_sem, halo_send, halo_recv, x_send, x_recv, y_send, y_recv,
     z_send, z_recv, g_send, g_recv, ay_send, ay_recv, ax_send, ax_recv, st_send, st_recv) = scratch
    count = dict(zip(AXES, dims))
    nx, ny, nz = dims
    plane_peers = nx * ny - 1
    me = {axis: lax.axis_index(axis) for axis in AXES}
    taps, rows, chan = raw_ref.shape
    ex, ey, ez = in_ref.shape[:3]
    padded_taps = send_z.shape[0]
    piece = padded_taps // nz
    fan_count = float(rows * nx * ny * taps)

    def peer(axis, k):
        return lax.rem(me[axis] + k, count[axis])

    def plane_peer(k):
        flat = lax.rem(me["gx"] * ny + me["gy"] + k, nx * ny)
        return {"gx": lax.div(flat, ny), "gy": lax.rem(flat, ny)}

    def remote(src, dst, send_sem, recv_sem, where):
        return pltpu.make_async_remote_copy(
            src_ref=src, dst_ref=dst, send_sem=send_sem, recv_sem=recv_sem,
            device_id=where, device_id_type=MESH,
        )

    def wait_all(copies):
        for copy in copies:
            copy.wait()

    body = pl.ds(1, ey)
    load_raw = pltpu.make_async_copy(raw_hbm, raw_ref, load_sem.at[0])
    load_cot = pltpu.make_async_copy(cot_hbm, shifted.at[1, pl.ds(1, ex), body], load_sem.at[1])
    load_in = pltpu.make_async_copy(in_hbm, in_ref, load_sem.at[2])
    load_raw.start()
    load_cot.start()
    load_in.start()

    barrier = pltpu.get_barrier_semaphore()
    for k in range(1, nx * ny):
        pl.semaphore_signal(barrier, inc=1, device_id=plane_peer(k), device_id_type=MESH)
    for k in range(1, nz):
        pl.semaphore_signal(barrier, inc=1, device_id={"gz": peer("gz", k)}, device_id_type=MESH)

    def exchange_start(slot, base, peers):
        copies = []
        for k, where in enumerate(peers):
            copy = remote(stats.at[slot], stats_in.at[base + k], st_send.at[base + k], st_recv.at[base + k], where)
            copy.start()
            copies.append(copy)
        return copies

    def exchange_sum(slot, base, copies):
        wait_all(copies)
        total = stats[slot]
        for k in range(len(copies)):
            total = total + stats_in[base + k]
        return total

    zero_plane = jnp.zeros((ey, ez, chan), BF16)
    zero_col = jnp.zeros((ex + 2, ez, chan), BF16)
    zero_face = jnp.zeros((ex + 2, ey + 2, chan), BF16)

    @pl.when(me["gx"] == 0)
    def _():
        shifted[1, 0, 1:ey + 1] = zero_plane

    @pl.when(me["gx"] == nx - 1)
    def _():
        shifted[1, ex + 1, 1:ey + 1] = zero_plane

    @pl.when(me["gy"] == 0)
    def _():
        shifted[1, :, 0] = zero_col

    @pl.when(me["gy"] == ny - 1)
    def _():
        shifted[1, :, ey + 1] = zero_col

    @pl.when(me["gz"] == 0)
    def _():
        face_in[0] = zero_face

    @pl.when(me["gz"] == nz - 1)
    def _():
        face_in[1] = zero_face

    for t in range(taps, padded_taps):
        send_z[t] = jnp.zeros((rows, chan), BF16)
        std[t] = jnp.zeros((rows, chan), F32)

    load_raw.wait()

    def per_output(value):
        return jnp.sum(jnp.sum(value, axis=0), axis=0, keepdims=True)

    raw = raw_ref[...]
    stats[0] = jnp.concatenate([per_output(raw), per_output(raw * raw), jnp.zeros((6, chan), F32)], axis=0)
    load_cot.wait()
    pl.semaphore_wait(barrier, plane_peers + nz - 1)

    def halo(axis, number, low_src, high_dst, high_src, low_dst):
        lower, upper = lax.max(me[axis] - 1, 0), lax.min(me[axis] + 1, count[axis] - 1)
        down = remote(low_src, high_dst, halo_send.at[2 * number], halo_recv.at[2 * number], {axis: lower})
        up = remote(high_src, low_dst, halo_send.at[2 * number + 1], halo_recv.at[2 * number + 1], {axis: upper})

        @pl.when(me[axis] > 0)
        def _():
            down.start()

        @pl.when(me[axis] < count[axis] - 1)
        def _():
            up.start()

        def finish():
            @pl.when(me[axis] > 0)
            def _():
                down.wait_send()
                up.wait_recv()

            @pl.when(me[axis] < count[axis] - 1)
            def _():
                up.wait_send()
                down.wait_recv()

        return finish

    halo_x = halo("gx", 0, shifted.at[1, 1, body], shifted.at[1, ex + 1, body],
                  shifted.at[1, ex, body], shifted.at[1, 0, body])
    weight_sums = exchange_start(0, 0, [plane_peer(k) for k in range(1, nx * ny)])
    load_in.wait()
    for x in range(ex):
        in_t[:, x * ey * ez:(x + 1) * ey * ez] = in_ref[x].reshape(ey * ez, chan).T
    halo_x()
    halo_y = halo("gy", 1, shifted.at[1, :, 1], shifted.at[1, :, ey + 1],
                  shifted.at[1, :, ey], shifted.at[1, :, 0])

    sums = exchange_sum(0, 0, weight_sums)
    mean_out = sums[0:1] / fan_count
    var_out = sums[1:2] / fan_count - mean_out * mean_out
    inv_std = lax.rsqrt(var_out + var_eps)
    order = [t for c in (1, 0, 2) for t in range(c, taps, 3)]
    own = std_all.at[me["gx"], me["gy"]]
    for u, t in enumerate(order):
        value = (raw_ref[t] - mean_out) * inv_std
        std[u] = value
        own[u] = value.astype(BF16)
    gather_y = []
    for k in range(1, ny):
        copy = remote(own, own, ay_send.at[k - 1], ay_recv.at[k - 1], {"gy": peer("gy", k)})
        copy.start()
        gather_y.append(copy)

    halo_y()
    for x in range(ex + 2):
        plane = shifted[1, x].astype(F32)
        face_out[0, x] = plane[:, 0, :].astype(BF16)
        face_out[1, x] = plane[:, ez - 1, :].astype(BF16)
    halo_z = halo("gz", 2, face_out.at[0], face_in.at[1], face_out.at[1], face_in.at[0])

    def view(t, start, planes):
        a, b, c = t // 9, (t // 3) % 3, t % 3
        block = shifted[2 - c, pl.ds(start + 2 - a, planes), 2 - b:2 - b + ey]
        return block.reshape(planes * ey * ez, chan)

    chunk = taps // 3

    def filter_chunk(n):
        for u in range(n * chunk, (n + 1) * chunk, 2):
            group = list(range(u, min(u + 2, (n + 1) * chunk)))
            views = [view(order[v], 0, ex) for v in group]
            right = jnp.concatenate(views, axis=1) if len(views) > 1 else views[0]
            product = jnp.dot(in_t[...], right, preferred_element_type=F32)
            for j, v in enumerate(group):
                for gx in range(nx):
                    for gy in range(ny):
                        low = (gx * ny + gy) * rows
                        part[gx, gy, v] = product[low:low + rows, j * chan:(j + 1) * chan]
        copies = []
        span = pl.ds(n * chunk, chunk)
        for k in range(1, nx):
            index = n * (nx - 1) + k - 1
            copy = remote(part.at[peer("gx", k), :, span], recv_x.at[k - 1, :, span],
                          x_send.at[index], x_recv.at[index], {"gx": peer("gx", k)})
            copy.start()
            copies.append(copy)
        return copies

    def rows_chunk(n, copies):
        wait_all(copies)
        span = pl.ds(n * chunk, chunk)
        for gy in range(ny):
            total = part[me["gx"], gy, span]
            for k in range(1, nx):
                total = total + recv_x[k - 1, gy, span]
            send_y[gy, span] = total.astype(BF16)
        sent = []
        for k in range(1, ny):
            index = n * (ny - 1) + k - 1
            copy = remote(send_y.at[peer("gy", k), span], recv_y.at[k - 1, span],
                          y_send.at[index], y_recv.at[index], {"gy": peer("gy", k)})
            copy.start()
            sent.append(copy)
        return sent

    depth_index = lax.broadcasted_iota(jnp.int32, (ey + 2, ez, chan), 1)

    def shift(slot, side, amount, edge):
        for x in range(ex + 2):
            plane = shifted[1, x].astype(F32)
            outer = face_in[side, x].astype(F32)[:, None, :]
            shifted[slot, x] = jnp.where(depth_index == edge, outer, pltpu.roll(plane, amount, 1)).astype(BF16)

    copies_0 = filter_chunk(0)
    halo_z()
    shift(2, 1, ez - 1, ez - 1)
    copies_1 = filter_chunk(1)
    reduce_y = rows_chunk(0, copies_0)
    shift(0, 0, 1, 0)
    copies_2 = filter_chunk(2)
    reduce_y += rows_chunk(1, copies_1)
    wait_all(gather_y)
    gather_x = []
    for k in range(1, nx):
        copy = remote(std_all.at[me["gx"]], std_all.at[me["gx"]], ax_send.at[k - 1], ax_recv.at[k - 1],
                      {"gx": peer("gx", k)})
        copy.start()
        gather_x.append(copy)
    reduce_y += rows_chunk(2, copies_2)

    wait_all(gather_x)
    for u in range(taps):
        w_cat[:, u * chan:(u + 1) * chan] = std_all[:, :, u].reshape(nx * ny * rows, chan)
    step = 2 if ex % 2 == 0 else 1

    def dx_step(n, carry):
        start = n * step
        left = jnp.concatenate([view(t, start, step) for t in order], axis=1)
        product = lax.dot_general(left, w_cat[...], (((1,), (1,)), ((), ())), preferred_element_type=F32)
        dx_ref[pl.ds(start, step)] = product.astype(BF16).reshape(step, ey, ez, chan)
        return carry

    half = ex // step // 2
    lax.fori_loop(0, half, dx_step, 0)

    wait_all(reduce_y)
    total = send_y[me["gy"]].astype(F32)
    for k in range(1, ny):
        total = total + recv_y[k - 1].astype(F32)
    send_z[0:taps] = total.astype(BF16)
    reduce_z = []
    for k in range(1, nz):
        copy = remote(send_z.at[pl.ds(peer("gz", k) * piece, piece)], recv_z.at[k - 1],
                      z_send.at[k - 1], z_recv.at[k - 1], {"gz": peer("gz", k)})
        copy.start()
        reduce_z.append(copy)

    lax.fori_loop(half, ex // step, dx_step, 0)

    wait_all(reduce_z)
    mine = pl.ds(me["gz"] * piece, piece)
    grad = send_z[mine].astype(F32)
    for k in range(1, nz):
        grad = grad + recv_z[k - 1].astype(F32)
    full[mine] = grad
    stats[1] = jnp.concatenate(
        [per_output(grad), per_output(grad * std[mine]), per_output(grad * grad), jnp.zeros((5, chan), F32)], axis=0
    )
    depth_peers = [{"gz": peer("gz", k)} for k in range(1, nz)]
    sums_z = exchange_start(1, plane_peers, depth_peers)
    gather_z = []
    for k in range(1, nz):
        copy = remote(full.at[mine], full.at[mine], g_send.at[k - 1], g_recv.at[k - 1], {"gz": peer("gz", k)})
        copy.start()
        gather_z.append(copy)
    stats[2] = exchange_sum(1, plane_peers, sums_z)
    sums_xy = exchange_start(2, plane_peers + nz - 1, [plane_peer(k) for k in range(1, nx * ny)])
    wait_all(gather_z)
    sums = exchange_sum(2, plane_peers + nz - 1, sums_xy)
    sum_grad, sum_cross, sum_square = sums[0:1], sums[1:2], sums[2:3]
    mean_grad = sum_grad / fan_count
    mean_cross = sum_cross / fan_count
    spread = sum_square - 2.0 * mean_grad * sum_grad - 2.0 * mean_cross * sum_cross
    spread = (
        spread
        + fan_count * mean_grad * mean_grad
        + fan_count * mean_cross * mean_cross * var_out / (var_out + var_eps)
    )
    square_sum = jnp.sum(inv_std * inv_std * spread, axis=1, keepdims=True)
    scale = jnp.minimum(1.0, clip_norm * lax.rsqrt(square_sum + norm_eps))
    factor = inv_std * scale
    for u, t in enumerate(order):
        wg_ref[t] = factor * (full[u] - mean_grad - std[u] * mean_cross)


def on_device(dims, raw_weight, inputs, cotangent):
    nx, ny, nz = dims
    rows, taps, chan = raw_weight.shape
    ex, ey, ez = inputs.shape[:3]
    padded_taps = -(-taps // nz) * nz
    piece = padded_taps // nz
    stat_slots = 2 * (nx * ny - 1) + nz - 1
    dma = pltpu.SemaphoreType.DMA

    def pair(n):
        return [dma((max(n, 1),)), dma((max(n, 1),))]

    scratch = [
        pltpu.VMEM((taps, rows, chan), F32),
        pltpu.VMEM(inputs.shape, BF16),
        pltpu.VMEM((3, ex + 2, ey + 2, ez, chan), BF16),
        pltpu.VMEM((2, ex + 2, ey + 2, chan), BF16),
        pltpu.VMEM((2, ex + 2, ey + 2, chan), BF16),
        pltpu.VMEM((chan, ex * ey * ez), BF16),
        pltpu.VMEM((nx, ny, taps, rows, chan), F32),
        pltpu.VMEM((nx - 1, ny, taps, rows, chan), F32),
        pltpu.VMEM((ny, taps, rows, chan), BF16),
        pltpu.VMEM((ny - 1, taps, rows, chan), BF16),
        pltpu.VMEM((padded_taps, rows, chan), BF16),
        pltpu.VMEM((nz - 1, piece, rows, chan), BF16),
        pltpu.VMEM((padded_taps, rows, chan), F32),
        pltpu.VMEM((padded_taps, rows, chan), F32),
        pltpu.VMEM((nx, ny, taps, rows, chan), BF16),
        pltpu.VMEM((chan, taps * chan), BF16),
        pltpu.VMEM((3, 8, chan), F32),
        pltpu.VMEM((stat_slots, 8, chan), F32),
        dma((3,)), *pair(6), *pair(3 * (nx - 1)), *pair(3 * (ny - 1)), *pair(nz - 1), *pair(nz - 1),
        *pair(ny - 1), *pair(nx - 1), *pair(stat_slots),
    ]
    vmem = pl.BlockSpec(memory_space=pltpu.VMEM)
    anywhere = pl.BlockSpec(memory_space=pl.ANY)
    input_grad, weight_grad = pl.pallas_call(
        functools.partial(kernel, dims),
        out_shape=(
            jax.ShapeDtypeStruct(cotangent.shape, BF16),
            jax.ShapeDtypeStruct((taps, rows, chan), F32),
        ),
        in_specs=[anywhere] * 3,
        out_specs=(vmem, vmem),
        scratch_shapes=scratch,
        compiler_params=pltpu.CompilerParams(
            collective_id=0, has_side_effects=True, vmem_limit_bytes=60 * 1024 * 1024
        ),
    )(jnp.transpose(raw_weight, (1, 0, 2)), inputs, cotangent)
    return input_grad, jnp.transpose(weight_grad, (1, 0, 2))


def solution(mesh):
    dims = tuple(mesh.shape[axis] for axis in AXES)
    in_specs = (P(("gx", "gy"), None, None), P("gx", "gy", "gz", None), P("gx", "gy", "gz", None))
    out_specs = (P("gx", "gy", "gz", None), P(("gx", "gy"), None, None))
    return jax.shard_map(
        functools.partial(on_device, dims), mesh=mesh, in_specs=in_specs, out_specs=out_specs, check_vma=False
    )
```

time: 45.8 us -> 38.4 us (0.84)
  Pallas kernels: 40.2 us -> 35 us
  local copies, waits for them, and re-layouts: 4.7 us -> 2.6 us
    pallas_call x1, Pallas kernels: 40.2 us -> 35 us  [on_device(): pl.pallas_call(functools.partial(kernel, dims), out_shape=(jax.ShapeDtype...]
    unnamed x6 -> x4, local copies, waits for them, and re-layouts: 3.88 us -> 2.6 us
    pallas_call x1 -> x0, local copies, waits for them, and re-layouts: 0.82 us -> none  [on_device(): pl.pallas_call(functools.partial(kernel, dims), out_shape=(jax.ShapeDtype...]
where the time goes in v2:
time: 38.4 us; the launch traced here: 38.3 us
  Pallas kernels  35 us (91%)
  local copies, waits for them, and re-layouts  2.6 us (7%)
  between operations  0.65 us (2%)
    pallas_call x1, Pallas kernels, on_device(): pl.pallas_call(functools.partial(kernel, dims), out_shape=(jax.ShapeDtype...  35 us
    unnamed x4, local copies, waits for them, and re-layouts  2.6 us

profile of v2, /device:TPU:0, one launch (start us, length us, event | category | flops | bytes accessed | tf_op | source)
XLA Modules:
  0.0 38.3 jit_solution(16513640073564178889)
XLA Ops:
  0.6 35.0 %shard_map.50 = (bf16[8,16,16,128]{3,2,1,0:T(8,128)(2,1)}, f32[27,16,128]{2,1,0:T(8,128)}) custom-call(f32[27,16,128]{2,1,0:T(8,128)} %bitcast.2, bf16[8,16,16,128]{3,2,1,0:T(8,128)(2,1)} %in_hbm.1, bf16[8,16,16,128]{3,2,1,0:T(8,128)(2,1)} %cot_hbm.1), custom_call_target="tpu_custom_call" | custom-call | tf_op jit(solution)/shard_map/pallas_call | solution.py:351
  35.7 0.0 copy-start
  35.7 1.9 %copy.7 = bf16[8,16,16,128]{3,2,1,0:T(8,128)(2,1)} copy(bf16[8,16,16,128]{3,2,1,0:T(8,128)(2,1)} %get-tuple-element.8) | data formatting | bytes 1048576
  37.6 0.0 copy-done
  37.6 0.7 %copy.8 = f32[16,27,128]{2,0,1:T(8,128)} copy(f32[16,27,128]{2,0,1:T(8,128)S(1)} %bitcast.3) | data formatting | bytes 442368
Async XLA Ops:
  35.7 1.9 %copy-start = (f32[27,16,128]{2,1,0:T(8,128)S(1)}, f32[27,16,128]{2,1,0:T(8,128)}, u32[]{:S(2)}) copy-start(f32[27,16,128]{2,1,0:T(8,128)} %get-tuple-element.5) | copy-start | bytes 663556

commit v3 on v2

--- a/solution.py
+++ b/solution.py
@@ -14,6 +14,12 @@
 BF16 = jnp.bfloat16
 MESH = pl.DeviceIdType.MESH
 AXES = ("gx", "gy", "gz")
+
+
+def z_groups(taps, nz):
+    chunk = taps // 3
+    sizes = [-(-2 * chunk // nz), -(-chunk // nz)]
+    return [(0, 0, 2 * chunk, sizes[0]), (sizes[0] * nz, 2 * chunk, chunk, sizes[1])]
 
 
 def kernel(dims, raw_hbm, in_hbm, cot_hbm, dx_ref, wg_ref, *scratch):
@@ -26,8 +32,8 @@
     me = {axis: lax.axis_index(axis) for axis in AXES}
     taps, rows, chan = raw_ref.shape
     ex, ey, ez = in_ref.shape[:3]
-    padded_taps = send_z.shape[0]
-    piece = padded_taps // nz
+    chunk = taps // 3
+    groups = z_groups(taps, nz)
     fan_count = float(rows * nx * ny * taps)
 
     def peer(axis, k):
@@ -76,17 +82,17 @@
             total = total + stats_in[base + k]
         return total
 
-    zero_plane = jnp.zeros((ey, ez, chan), BF16)
+    zero_plane = jnp.zeros((ey + 2, ez, chan), BF16)
     zero_col = jnp.zeros((ex + 2, ez, chan), BF16)
     zero_face = jnp.zeros((ex + 2, ey + 2, chan), BF16)
 
     @pl.when(me["gx"] == 0)
     def _():
-        shifted[1, 0, 1:ey + 1] = zero_plane
+        shifted[1, 0] = zero_plane
 
     @pl.when(me["gx"] == nx - 1)
     def _():
-        shifted[1, ex + 1, 1:ey + 1] = zero_plane
+        shifted[1, ex + 1] = zero_plane
 
     @pl.when(me["gy"] == 0)
     def _():
@@ -104,7 +110,7 @@
     def _():
         face_in[1] = zero_face
 
-    for t in range(taps, padded_taps):
+    for t in [b + v for b, first, many, size in groups for v in range(many, size * nz)]:
         send_z[t] = jnp.zeros((rows, chan), BF16)
         std[t] = jnp.zeros((rows, chan), F32)
 
@@ -144,25 +150,40 @@
 
         return finish
 
-    halo_x = halo("gx", 0, shifted.at[1, 1, body], shifted.at[1, ex + 1, body],
-                  shifted.at[1, ex, body], shifted.at[1, 0, body])
+    def inside(dx, dy):
+        gx, gy = me["gx"] + dx, me["gy"] + dy
+        within = jnp.logical_and(gx >= 0, gx < nx)
+        return jnp.logical_and(within, jnp.logical_and(gy >= 0, gy < ny))
+
+    plane_halo = []
+    for dx, dy in [(0, -1), (0, 1), (-1, 0), (1, 0), (-1, -1), (-1, 1), (1, -1), (1, 1)]:
+        src_x = {-1: 1, 0: pl.ds(1, ex), 1: ex}[dx]
+        dst_x = {-1: ex + 1, 0: pl.ds(1, ex), 1: 0}[dx]
+        src_y = {-1: 1, 0: body, 1: ey}[dy]
+        dst_y = {-1: ey + 1, 0: body, 1: 0}[dy]
+        where = {
+            "gx": lax.min(lax.max(me["gx"] + dx, 0), nx - 1),
+            "gy": lax.min(lax.max(me["gy"] + dy, 0), ny - 1),
+        }
+        number = 2 + len(plane_halo)
+        copy = remote(shifted.at[1, src_x, src_y], shifted.at[1, dst_x, dst_y],
+                      halo_send.at[number], halo_recv.at[number], where)
+        pl.when(inside(dx, dy))(copy.start)
+        plane_halo.append((dx, dy, copy))
     weight_sums = exchange_start(0, 0, [plane_peer(k) for k in range(1, nx * ny)])
     load_in.wait()
     for x in range(ex):
         in_t[:, x * ey * ez:(x + 1) * ey * ez] = in_ref[x].reshape(ey * ez, chan).T
-    halo_x()
-    halo_y = halo("gy", 1, shifted.at[1, :, 1], shifted.at[1, :, ey + 1],
-                  shifted.at[1, :, ey], shifted.at[1, :, 0])
-
     sums = exchange_sum(0, 0, weight_sums)
     mean_out = sums[0:1] / fan_count
     var_out = sums[1:2] / fan_count - mean_out * mean_out
     inv_std = lax.rsqrt(var_out + var_eps)
     order = [t for c in (1, 0, 2) for t in range(c, taps, 3)]
+    slots = [b + v for b, first, many, size in groups for v in range(many)]
     own = std_all.at[me["gx"], me["gy"]]
     for u, t in enumerate(order):
         value = (raw_ref[t] - mean_out) * inv_std
-        std[u] = value
+        std[slots[u]] = value
         own[u] = value.astype(BF16)
     gather_y = []
     for k in range(1, ny):
@@ -170,19 +191,19 @@
         copy.start()
         gather_y.append(copy)
 
-    halo_y()
+    for dx, dy, copy in plane_halo:
+        pl.when(inside(dx, dy))(copy.wait_send)
+        pl.when(inside(-dx, -dy))(copy.wait_recv)
     for x in range(ex + 2):
         plane = shifted[1, x].astype(F32)
         face_out[0, x] = plane[:, 0, :].astype(BF16)
         face_out[1, x] = plane[:, ez - 1, :].astype(BF16)
-    halo_z = halo("gz", 2, face_out.at[0], face_in.at[1], face_out.at[1], face_in.at[0])
+    halo_z = halo("gz", 0, face_out.at[0], face_in.at[1], face_out.at[1], face_in.at[0])
 
     def view(t, start, planes):
         a, b, c = t // 9, (t // 3) % 3, t % 3
         block = shifted[2 - c, pl.ds(start + 2 - a, planes), 2 - b:2 - b + ey]
         return block.reshape(planes * ey * ez, chan)
-
-    chunk = taps // 3
 
     def filter_chunk(n):
         for u in range(n * chunk, (n + 1) * chunk, 2):
@@ -234,10 +255,10 @@
     halo_z()
     shift(2, 1, ez - 1, ez - 1)
     copies_1 = filter_chunk(1)
-    reduce_y = rows_chunk(0, copies_0)
+    reduce_y = [rows_chunk(0, copies_0)]
     shift(0, 0, 1, 0)
     copies_2 = filter_chunk(2)
-    reduce_y += rows_chunk(1, copies_1)
+    reduce_y.append(rows_chunk(1, copies_1))
     wait_all(gather_y)
     gather_x = []
     for k in range(1, nx):
@@ -245,7 +266,7 @@
                       {"gx": peer("gx", k)})
         copy.start()
         gather_x.append(copy)
-    reduce_y += rows_chunk(2, copies_2)
+    reduce_y.append(rows_chunk(2, copies_2))
 
     wait_all(gather_x)
     for u in range(taps):
@@ -259,39 +280,61 @@
         dx_ref[pl.ds(start, step)] = product.astype(BF16).reshape(step, ey, ez, chan)
         return carry
 
-    half = ex // step // 2
-    lax.fori_loop(0, half, dx_step, 0)
-
-    wait_all(reduce_y)
-    total = send_y[me["gy"]].astype(F32)
-    for k in range(1, ny):
-        total = total + recv_y[k - 1].astype(F32)
-    send_z[0:taps] = total.astype(BF16)
-    reduce_z = []
-    for k in range(1, nz):
-        copy = remote(send_z.at[pl.ds(peer("gz", k) * piece, piece)], recv_z.at[k - 1],
-                      z_send.at[k - 1], z_recv.at[k - 1], {"gz": peer("gz", k)})
-        copy.start()
-        reduce_z.append(copy)
-
-    lax.fori_loop(half, ex // step, dx_step, 0)
-
-    wait_all(reduce_z)
-    mine = pl.ds(me["gz"] * piece, piece)
-    grad = send_z[mine].astype(F32)
-    for k in range(1, nz):
-        grad = grad + recv_z[k - 1].astype(F32)
-    full[mine] = grad
-    stats[1] = jnp.concatenate(
-        [per_output(grad), per_output(grad * std[mine]), per_output(grad * grad), jnp.zeros((5, chan), F32)], axis=0
-    )
+    steps = ex // step
+    marks = [0, steps // 4, steps * 3 // 4, steps]
+
+    def depth_start(g):
+        base, first, many, size = groups[g]
+        span = pl.ds(first, many)
+        total = send_y[me["gy"], span].astype(F32)
+        for k in range(1, ny):
+            total = total + recv_y[k - 1, span].astype(F32)
+        send_z[base:base + many] = total.astype(BF16)
+        copies = []
+        for k in range(1, nz):
+            index = g * (nz - 1) + k - 1
+            copy = remote(send_z.at[pl.ds(base + peer("gz", k) * size, size)],
+                          recv_z.at[k - 1, pl.ds(base // nz, size)],
+                          z_send.at[index], z_recv.at[index], {"gz": peer("gz", k)})
+            copy.start()
+            copies.append(copy)
+        return copies
+
+    def depth_sum(g, copies):
+        wait_all(copies)
+        base, first, many, size = groups[g]
+        mine = pl.ds(base + me["gz"] * size, size)
+        grad = send_z[mine].astype(F32)
+        for k in range(1, nz):
+            grad = grad + recv_z[k - 1, pl.ds(base // nz, size)].astype(F32)
+        full[mine] = grad.astype(BF16)
+        sums = [per_output(grad), per_output(grad * std[mine]), per_output(grad * grad)]
+        return jnp.concatenate(sums + [jnp.zeros((5, chan), F32)], axis=0)
+
+    def gather_start(g):
+        base, first, many, size = groups[g]
+        mine = pl.ds(base + me["gz"] * size, size)
+        copies = []
+        for k in range(1, nz):
+            index = g * (nz - 1) + k - 1
+            copy = remote(full.at[mine], full.at[mine], g_send.at[index], g_recv.at[index], {"gz": peer("gz", k)})
+            copy.start()
+            copies.append(copy)
+        return copies
+
+    lax.fori_loop(marks[0], marks[1], dx_step, 0)
+    wait_all(reduce_y[0] + reduce_y[1])
+    reduce_0 = depth_start(0)
+    lax.fori_loop(marks[1], marks[2], dx_step, 0)
+    wait_all(reduce_y[2])
+    reduce_1 = depth_start(1)
+    lax.fori_loop(marks[2], marks[3], dx_step, 0)
+    first_sums = depth_sum(0, reduce_0)
+    gather_z = gather_start(0)
+    stats[1] = first_sums + depth_sum(1, reduce_1)
     depth_peers = [{"gz": peer("gz", k)} for k in range(1, nz)]
     sums_z = exchange_start(1, plane_peers, depth_peers)
-    gather_z = []
-    for k in range(1, nz):
-        copy = remote(full.at[mine], full.at[mine], g_send.at[k - 1], g_recv.at[k - 1], {"gz": peer("gz", k)})
-        copy.start()
-        gather_z.append(copy)
+    gather_z += gather_start(1)
     stats[2] = exchange_sum(1, plane_peers, sums_z)
     sums_xy = exchange_start(2, plane_peers + nz - 1, [plane_peer(k) for k in range(1, nx * ny)])
     wait_all(gather_z)
@@ -309,15 +352,17 @@
     scale = jnp.minimum(1.0, clip_norm * lax.rsqrt(square_sum + norm_eps))
     factor = inv_std * scale
     for u, t in enumerate(order):
-        wg_ref[t] = factor * (full[u] - mean_grad - std[u] * mean_cross)
+        value = full[slots[u]].astype(F32)
+        wg_ref[t] = factor * (value - mean_grad - std[slots[u]] * mean_cross)
 
 
 def on_device(dims, raw_weight, inputs, cotangent):
     nx, ny, nz = dims
     rows, taps, chan = raw_weight.shape
     ex, ey, ez = inputs.shape[:3]
-    padded_taps = -(-taps // nz) * nz
-    piece = padded_taps // nz
+    groups = z_groups(taps, nz)
+    piece = sum(size for base, first, many, size in groups)
+    padded_taps = piece * nz
     stat_slots = 2 * (nx * ny - 1) + nz - 1
     dma = pltpu.SemaphoreType.DMA
 
@@ -337,13 +382,13 @@
         pltpu.VMEM((ny - 1, taps, rows, chan), BF16),
         pltpu.VMEM((padded_taps, rows, chan), BF16),
         pltpu.VMEM((nz - 1, piece, rows, chan), BF16),
-        pltpu.VMEM((padded_taps, rows, chan), F32),
+        pltpu.VMEM((padded_taps, rows, chan), BF16),
         pltpu.VMEM((padded_taps, rows, chan), F32),
         pltpu.VMEM((nx, ny, taps, rows, chan), BF16),
         pltpu.VMEM((chan, taps * chan), BF16),
         pltpu.VMEM((3, 8, chan), F32),
         pltpu.VMEM((stat_slots, 8, chan), F32),
-        dma((3,)), *pair(6), *pair(3 * (nx - 1)), *pair(3 * (ny - 1)), *pair(nz - 1), *pair(nz - 1),
+        dma((3,)), *pair(10), *pair(3 * (nx - 1)), *pair(3 * (ny - 1)), *pair(2 * (nz - 1)), *pair(2 * (nz - 1)),
         *pair(ny - 1), *pair(nx - 1), *pair(stat_slots),
     ]
     vmem = pl.BlockSpec(memory_space=pltpu.VMEM)

time: 38.4 us -> 38.3 us (level)
  no operation moved by 1% of the time
where the time goes in v3:
time: 38.3 us; the launch traced here: 38.2 us
  Pallas kernels  34.9 us (91%)
  local copies, waits for them, and re-layouts  2.6 us (7%)
  between operations  0.65 us (2%)
    pallas_call x1, Pallas kernels, on_device(): pl.pallas_call(functools.partial(kernel, dims), out_shape=(jax.ShapeDtype...  34.9 us
    unnamed x4, local copies, waits for them, and re-layouts  2.6 us

profile of v3, /device:TPU:0, one launch (start us, length us, event | category | flops | bytes accessed | tf_op | source)
XLA Modules:
  0.0 38.2 jit_solution(4154020711629222060)
XLA Ops:
  0.6 34.9 %shard_map.50 = (bf16[8,16,16,128]{3,2,1,0:T(8,128)(2,1)}, f32[27,16,128]{2,1,0:T(8,128)}) custom-call(f32[27,16,128]{2,1,0:T(8,128)} %bitcast.2, bf16[8,16,16,128]{3,2,1,0:T(8,128)(2,1)} %in_hbm.1, bf16[8,16,16,128]{3,2,1,0:T(8,128)(2,1)} %cot_hbm.1), custom_call_target="tpu_custom_call" | custom-call | tf_op jit(solution)/shard_map/pallas_call | solution.py:396
  35.6 0.0 copy-start
  35.6 1.9 %copy.7 = bf16[8,16,16,128]{3,2,1,0:T(8,128)(2,1)} copy(bf16[8,16,16,128]{3,2,1,0:T(8,128)(2,1)} %get-tuple-element.8) | data formatting | bytes 1048576
  37.5 0.0 copy-done
  37.5 0.7 %copy.8 = f32[16,27,128]{2,0,1:T(8,128)} copy(f32[16,27,128]{2,0,1:T(8,128)S(1)} %bitcast.3) | data formatting | bytes 442368
Async XLA Ops:
  35.6 1.9 %copy-start = (f32[27,16,128]{2,1,0:T(8,128)S(1)}, f32[27,16,128]{2,1,0:T(8,128)}, u32[]{:S(2)}) copy-start(f32[27,16,128]{2,1,0:T(8,128)} %get-tuple-element.5) | copy-start | bytes 663556

commit v4 on v3

--- a/solution.py
+++ b/solution.py
@@ -24,8 +24,8 @@
 
 def kernel(dims, raw_hbm, in_hbm, cot_hbm, dx_ref, wg_ref, *scratch):
     (raw_ref, in_ref, shifted, face_out, face_in, in_t, part, recv_x, send_y, recv_y, send_z, recv_z, full, std,
-     std_all, w_cat, stats, stats_in, load_sem, halo_send, halo_recv, x_send, x_recv, y_send, y_recv,
-     z_send, z_recv, g_send, g_recv, ay_send, ay_recv, ax_send, ax_recv, st_send, st_recv) = scratch
+     std_all, w_cat, stats, stats_in, total_in, load_sem, halo_send, halo_recv, x_send, x_recv, y_send, y_recv,
+     z_send, z_recv, g_send, g_recv, ay_send, ay_recv, ax_send, ax_recv, st_send, st_recv, t_send, t_recv) = scratch
     count = dict(zip(AXES, dims))
     nx, ny, nz = dims
     plane_peers = nx * ny - 1
@@ -121,8 +121,9 @@
 
     raw = raw_ref[...]
     stats[0] = jnp.concatenate([per_output(raw), per_output(raw * raw), jnp.zeros((6, chan), F32)], axis=0)
+    pl.semaphore_wait(barrier, plane_peers + nz - 1)
+    weight_sums = exchange_start(0, 0, [plane_peer(k) for k in range(1, nx * ny)])
     load_cot.wait()
-    pl.semaphore_wait(barrier, plane_peers + nz - 1)
 
     def halo(axis, number, low_src, high_dst, high_src, low_dst):
         lower, upper = lax.max(me[axis] - 1, 0), lax.min(me[axis] + 1, count[axis] - 1)
@@ -170,10 +171,18 @@
                       halo_send.at[number], halo_recv.at[number], where)
         pl.when(inside(dx, dy))(copy.start)
         plane_halo.append((dx, dy, copy))
-    weight_sums = exchange_start(0, 0, [plane_peer(k) for k in range(1, nx * ny)])
     load_in.wait()
     for x in range(ex):
         in_t[:, x * ey * ez:(x + 1) * ey * ez] = in_ref[x].reshape(ey * ez, chan).T
+    for dx, dy, copy in plane_halo:
+        pl.when(inside(dx, dy))(copy.wait_send)
+        pl.when(inside(-dx, -dy))(copy.wait_recv)
+    for x in range(ex + 2):
+        plane = shifted[1, x].astype(F32)
+        face_out[0, x] = plane[:, 0, :].astype(BF16)
+        face_out[1, x] = plane[:, ez - 1, :].astype(BF16)
+    halo_z = halo("gz", 0, face_out.at[0], face_in.at[1], face_out.at[1], face_in.at[0])
+
     sums = exchange_sum(0, 0, weight_sums)
     mean_out = sums[0:1] / fan_count
     var_out = sums[1:2] / fan_count - mean_out * mean_out
@@ -190,15 +199,6 @@
         copy = remote(own, own, ay_send.at[k - 1], ay_recv.at[k - 1], {"gy": peer("gy", k)})
         copy.start()
         gather_y.append(copy)
-
-    for dx, dy, copy in plane_halo:
-        pl.when(inside(dx, dy))(copy.wait_send)
-        pl.when(inside(-dx, -dy))(copy.wait_recv)
-    for x in range(ex + 2):
-        plane = shifted[1, x].astype(F32)
-        face_out[0, x] = plane[:, 0, :].astype(BF16)
-        face_out[1, x] = plane[:, ez - 1, :].astype(BF16)
-    halo_z = halo("gz", 0, face_out.at[0], face_in.at[1], face_out.at[1], face_in.at[0])
 
     def view(t, start, planes):
         a, b, c = t // 9, (t // 3) % 3, t % 3
@@ -259,6 +259,7 @@
     shift(0, 0, 1, 0)
     copies_2 = filter_chunk(2)
     reduce_y.append(rows_chunk(1, copies_1))
+    reduce_y.append(rows_chunk(2, copies_2))
     wait_all(gather_y)
     gather_x = []
     for k in range(1, nx):
@@ -266,11 +267,7 @@
                       {"gx": peer("gx", k)})
         copy.start()
         gather_x.append(copy)
-    reduce_y.append(rows_chunk(2, copies_2))
-
-    wait_all(gather_x)
-    for u in range(taps):
-        w_cat[:, u * chan:(u + 1) * chan] = std_all[:, :, u].reshape(nx * ny * rows, chan)
+
     step = 2 if ex % 2 == 0 else 1
 
     def dx_step(n, carry):
@@ -281,7 +278,7 @@
         return carry
 
     steps = ex // step
-    marks = [0, steps // 4, steps * 3 // 4, steps]
+    half = steps // 2
 
     def depth_start(g):
         base, first, many, size = groups[g]
@@ -322,23 +319,37 @@
             copies.append(copy)
         return copies
 
-    lax.fori_loop(marks[0], marks[1], dx_step, 0)
     wait_all(reduce_y[0] + reduce_y[1])
     reduce_0 = depth_start(0)
-    lax.fori_loop(marks[1], marks[2], dx_step, 0)
+    wait_all(gather_x)
+    for u in range(taps):
+        w_cat[:, u * chan:(u + 1) * chan] = std_all[:, :, u].reshape(nx * ny * rows, chan)
+    lax.fori_loop(0, half, dx_step, 0)
     wait_all(reduce_y[2])
     reduce_1 = depth_start(1)
-    lax.fori_loop(marks[2], marks[3], dx_step, 0)
+    lax.fori_loop(half, steps, dx_step, 0)
     first_sums = depth_sum(0, reduce_0)
     gather_z = gather_start(0)
     stats[1] = first_sums + depth_sum(1, reduce_1)
-    depth_peers = [{"gz": peer("gz", k)} for k in range(1, nz)]
-    sums_z = exchange_start(1, plane_peers, depth_peers)
+    flat = (me["gx"] * ny + me["gy"]) * nz + me["gz"]
+    total_in[flat] = stats[1]
+    final_sums = []
+    for k in range(1, nx * ny * nz):
+        other = lax.rem(flat + k, nx * ny * nz)
+        where = {
+            "gx": lax.div(other, ny * nz),
+            "gy": lax.rem(lax.div(other, nz), ny),
+            "gz": lax.rem(other, nz),
+        }
+        copy = remote(stats.at[1], total_in.at[flat], t_send.at[k - 1], t_recv.at[k - 1], where)
+        copy.start()
+        final_sums.append(copy)
     gather_z += gather_start(1)
-    stats[2] = exchange_sum(1, plane_peers, sums_z)
-    sums_xy = exchange_start(2, plane_peers + nz - 1, [plane_peer(k) for k in range(1, nx * ny)])
+    wait_all(final_sums)
+    sums = total_in[0]
+    for k in range(1, nx * ny * nz):
+        sums = sums + total_in[k]
     wait_all(gather_z)
-    sums = exchange_sum(2, plane_peers + nz - 1, sums_xy)
     sum_grad, sum_cross, sum_square = sums[0:1], sums[1:2], sums[2:3]
     mean_grad = sum_grad / fan_count
     mean_cross = sum_cross / fan_count
@@ -363,7 +374,7 @@
     groups = z_groups(taps, nz)
     piece = sum(size for base, first, many, size in groups)
     padded_taps = piece * nz
-    stat_slots = 2 * (nx * ny - 1) + nz - 1
+    stat_slots = nx * ny - 1
     dma = pltpu.SemaphoreType.DMA
 
     def pair(n):
@@ -386,10 +397,11 @@
         pltpu.VMEM((padded_taps, rows, chan), F32),
         pltpu.VMEM((nx, ny, taps, rows, chan), BF16),
         pltpu.VMEM((chan, taps * chan), BF16),
-        pltpu.VMEM((3, 8, chan), F32),
+        pltpu.VMEM((2, 8, chan), F32),
         pltpu.VMEM((stat_slots, 8, chan), F32),
+        pltpu.VMEM((nx * ny * nz, 8, chan), F32),
         dma((3,)), *pair(10), *pair(3 * (nx - 1)), *pair(3 * (ny - 1)), *pair(2 * (nz - 1)), *pair(2 * (nz - 1)),
-        *pair(ny - 1), *pair(nx - 1), *pair(stat_slots),
+        *pair(ny - 1), *pair(nx - 1), *pair(stat_slots), *pair(nx * ny * nz - 1),
     ]
     vmem = pl.BlockSpec(memory_space=pltpu.VMEM)
     anywhere = pl.BlockSpec(memory_space=pl.ANY)

time: 38.3 us -> 37.6 us (0.982)
  Pallas kernels: 34.9 us -> 34.2 us
    pallas_call x1, Pallas kernels: 34.9 us -> 34.2 us  [on_device(): pl.pallas_call(functools.partial(kernel, dims), out_shape=(jax.ShapeDtype...]
where the time goes in v4:
time: 37.6 us; the launch traced here: 37.5 us
  Pallas kernels  34.2 us (91%)
  local copies, waits for them, and re-layouts  2.6 us (7%)
  between operations  0.65 us (2%)
    pallas_call x1, Pallas kernels, on_device(): pl.pallas_call(functools.partial(kernel, dims), out_shape=(jax.ShapeDtype...  34.2 us
    unnamed x4, local copies, waits for them, and re-layouts  2.6 us

profile of v4, /device:TPU:0, one launch (start us, length us, event | category | flops | bytes accessed | tf_op | source)
XLA Modules:
  0.0 37.5 jit_solution(5211112686576529303)
XLA Ops:
  0.6 34.2 %shard_map.50 = (bf16[8,16,16,128]{3,2,1,0:T(8,128)(2,1)}, f32[27,16,128]{2,1,0:T(8,128)}) custom-call(f32[27,16,128]{2,1,0:T(8,128)} %bitcast.2, bf16[8,16,16,128]{3,2,1,0:T(8,128)(2,1)} %in_hbm.1, bf16[8,16,16,128]{3,2,1,0:T(8,128)(2,1)} %cot_hbm.1), custom_call_target="tpu_custom_call" | custom-call | tf_op jit(solution)/shard_map/pallas_call | solution.py:408
  34.9 0.0 copy-start
  34.9 1.9 %copy.7 = bf16[8,16,16,128]{3,2,1,0:T(8,128)(2,1)} copy(bf16[8,16,16,128]{3,2,1,0:T(8,128)(2,1)} %get-tuple-element.8) | data formatting | bytes 1048576
  36.8 0.0 copy-done
  36.8 0.7 %copy.8 = f32[16,27,128]{2,0,1:T(8,128)} copy(f32[16,27,128]{2,0,1:T(8,128)S(1)} %bitcast.3) | data formatting | bytes 442368
Async XLA Ops:
  34.9 1.9 %copy-start = (f32[27,16,128]{2,1,0:T(8,128)S(1)}, f32[27,16,128]{2,1,0:T(8,128)}, u32[]{:S(2)}) copy-start(f32[27,16,128]{2,1,0:T(8,128)} %get-tuple-element.5) | copy-start | bytes 663556

commit v5 on v4

--- a/solution.py
+++ b/solution.py
@@ -319,12 +319,12 @@
             copies.append(copy)
         return copies
 
-    wait_all(reduce_y[0] + reduce_y[1])
-    reduce_0 = depth_start(0)
     wait_all(gather_x)
     for u in range(taps):
         w_cat[:, u * chan:(u + 1) * chan] = std_all[:, :, u].reshape(nx * ny * rows, chan)
     lax.fori_loop(0, half, dx_step, 0)
+    wait_all(reduce_y[0] + reduce_y[1])
+    reduce_0 = depth_start(0)
     wait_all(reduce_y[2])
     reduce_1 = depth_start(1)
     lax.fori_loop(half, steps, dx_step, 0)

time: 37.6 us -> 38.6 us (1.027)
  Pallas kernels: 34.2 us -> 35.2 us
    pallas_call x1, Pallas kernels: 34.2 us -> 35.2 us  [on_device(): pl.pallas_call(functools.partial(kernel, dims), out_shape=(jax.ShapeDtype...]
where the time goes in v5:
time: 38.6 us; the launch traced here: 38.5 us
  Pallas kernels  35.2 us (91%)
  local copies, waits for them, and re-layouts  2.6 us (7%)
  between operations  0.65 us (2%)
    pallas_call x1, Pallas kernels, on_device(): pl.pallas_call(functools.partial(kernel, dims), out_shape=(jax.ShapeDtype...  35.2 us
    unnamed x4, local copies, waits for them, and re-layouts  2.6 us

profile of v5, /device:TPU:0, one launch (start us, length us, event | category | flops | bytes accessed | tf_op | source)
XLA Modules:
  0.0 38.5 jit_solution(18396062021679168132)
XLA Ops:
  0.6 35.2 %shard_map.50 = (bf16[8,16,16,128]{3,2,1,0:T(8,128)(2,1)}, f32[27,16,128]{2,1,0:T(8,128)}) custom-call(f32[27,16,128]{2,1,0:T(8,128)} %bitcast.2, bf16[8,16,16,128]{3,2,1,0:T(8,128)(2,1)} %in_hbm.1, bf16[8,16,16,128]{3,2,1,0:T(8,128)(2,1)} %cot_hbm.1), custom_call_target="tpu_custom_call" | custom-call | tf_op jit(solution)/shard_map/pallas_call | solution.py:408
  35.9 0.0 copy-start
  35.9 1.9 %copy.7 = bf16[8,16,16,128]{3,2,1,0:T(8,128)(2,1)} copy(bf16[8,16,16,128]{3,2,1,0:T(8,128)(2,1)} %get-tuple-element.8) | data formatting | bytes 1048576
  37.8 0.0 copy-done
  37.8 0.7 %copy.8 = f32[16,27,128]{2,0,1:T(8,128)} copy(f32[16,27,128]{2,0,1:T(8,128)S(1)} %bitcast.3) | data formatting | bytes 442368
Async XLA Ops:
  35.9 1.9 %copy-start = (f32[27,16,128]{2,1,0:T(8,128)S(1)}, f32[27,16,128]{2,1,0:T(8,128)}, u32[]{:S(2)}) copy-start(f32[27,16,128]{2,1,0:T(8,128)} %get-tuple-element.5) | copy-start | bytes 663556
